TPU v7x, 32 devices: a whole 2x2x4 slice. The times are simulated.
32 devices in a mesh: groups: 2 (over y), expert: 4 (over z), mp: 4 (over x, core).
Axes of the slice: x: 2, y: 2, z: 4, core: 2. Of those that a mesh axis runs over, the one named last changes fastest.
Arguments:
- tokens: bfloat16 [6144, 1024], P(('groups', 'expert'), 'mp'), parts along dimension 0, may hold values from -60 to 60
- gain: float32 [1024], replicated, may hold values from 0.1 to 1.9
- w_res_in: bfloat16 [1024, 4096], P(None, 'mp'), may hold values from -0.1875 to 0.1875
- w_res_out: bfloat16 [4096, 1024], P('mp'), may hold values from -0.09375 to 0.09375
- w_exp_in: bfloat16 [4, 1024, 4096], P('expert', None, 'mp'), may hold values from -0.1875 to 0.1875
- w_exp_out: bfloat16 [4, 4096, 1024], P('expert', 'mp'), may hold values from -0.09375 to 0.09375
- expert_of: int32 [6144], P(('groups', 'expert')), parts along dimension 0, may hold values from 0 to 3
- slot_of: int32 [6144], P(('groups', 'expert')), parts along dimension 0, may hold values from -1 to 239, as said below
- gate_prob: float32 [6144], P(('groups', 'expert')), parts along dimension 0, may hold values from 0.2 to 1
Outputs:
- layer_out: bfloat16 [6144, 1024], P(('groups', 'expert'), 'mp'), parts along dimension 0
There are 2 independent parts, one for each index of `groups`. A program takes and returns all parts, laid end to end along the dimension named above; an argument that names none is the same for every part. Nothing has to cross between parts.
Inputs may be any that keep to these rules, and one draw needn't show every extreme that they name: slot_of[t] is the number of earlier tokens of t's aligned block of 768 tokens with the same expert_of, or -1 where that number is 240 or more. In every draw one expert has more than 240 tokens in every aligned block.
All inputs are finite; a program needn't handle non-finite values.
Results may differ from a plain program's by a relative error of at most 0.014.
Values may be sent and summed in bfloat16 or wider, within the bound.
A program may use at most 64 MiB of HBM per device.

v0:
```python
import functools

import jax
import jax.numpy as jnp
from jax import lax
from jax.experimental import pallas as pl
from jax.experimental.pallas import tpu as pltpu
from jax.sharding import PartitionSpec as P


def rms_rows(tokens, gain):
    values = tokens.astype(jnp.float32)
    inverse = lax.rsqrt(jnp.mean(values * values, axis=-1, keepdims=True) + 1e-05)
    return (values * inverse * gain).astype(jnp.bfloat16)


def per_device(
    tokens, gain, w_res_in, w_res_out, w_exp_in, w_exp_out, expert_of, slot_of, gate_prob
):
    full_rows = lax.all_gather(tokens, "mp", axis=1, tiled=True)
    normed = rms_rows(full_rows, gain)
    res_hidden = jax.nn.gelu(jnp.dot(normed, w_res_in, preferred_element_type=jnp.float32)).astype(
        jnp.bfloat16
    )
    res_part = jnp.dot(res_hidden, w_res_out, preferred_element_type=jnp.float32)
    row_count = expert_of.shape[0]
    experts = lax.axis_size("expert")
    capacity = max(2, 5 * row_count // (4 * experts))
    feat_width = tokens.shape[1]
    slot_id = jnp.where(slot_of >= 0, expert_of * capacity + slot_of, -1)
    slot_index = jnp.arange(experts * capacity, dtype=jnp.int32)
    send_table = (slot_index[:, None] == slot_id[None, :]).astype(jnp.bfloat16)
    take_table = (slot_id[:, None] == slot_index[None, :]).astype(jnp.bfloat16)
    local_in = w_exp_in[0]
    local_out = w_exp_out[0]
    mp_index = lax.axis_index("mp")
    own_slice = lax.dynamic_slice_in_dim(normed, mp_index * feat_width, feat_width, 1)
    outgoing = jnp.dot(send_table, own_slice, preferred_element_type=jnp.float32).astype(
        jnp.bfloat16
    )
    incoming = lax.all_to_all(
        outgoing.reshape(experts, capacity, feat_width),
        "expert",
        split_axis=0,
        concat_axis=0,
        tiled=True,
    )
    piece = lax.all_gather(incoming, "mp", axis=2, tiled=True)
    flat_piece = piece.reshape(-1, piece.shape[2])
    preact = jnp.dot(flat_piece, local_in, preferred_element_type=jnp.float32)
    exp_hidden = jax.nn.gelu(preact).astype(jnp.bfloat16)
    exp_part = jnp.dot(exp_hidden, local_out, preferred_element_type=jnp.float32)
    gate_column = gate_prob[:, None]
    summed = lax.psum_scatter(exp_part.astype(jnp.bfloat16), "mp", scatter_dimension=1, tiled=True)
    returned = lax.all_to_all(
        summed.reshape(experts, capacity, feat_width),
        "expert",
        split_axis=0,
        concat_axis=0,
        tiled=True,
    )
    moe_value = jnp.dot(
        take_table,
        returned.reshape(experts * capacity, feat_width),
        preferred_element_type=jnp.float32,
    )
    res_sum = lax.psum_scatter(
        res_part.astype(jnp.bfloat16), "mp", scatter_dimension=1, tiled=True
    ).astype(jnp.float32)
    return (res_sum + gate_column * moe_value).astype(jnp.bfloat16)


MESH = pl.DeviceIdType.MESH
F32 = jnp.float32
BF16 = jnp.bfloat16


def dot(a, b):
    return jnp.dot(a, b, preferred_element_type=F32)


def first_layer(rows_ref, w_ref, hidden_ref, chunk, lo, size):
    def body(n, carry):
        cols = pl.ds(pl.multiple_of(n * chunk, chunk), chunk)
        hidden_ref[lo:lo + size, cols] = jax.nn.gelu(dot(rows_ref[lo:lo + size], w_ref[:, cols])).astype(BF16)
        return carry

    lax.fori_loop(0, hidden_ref.shape[1] // chunk, body, 0)


def fused_kernel(
    halves, tokens, gain, w_ri_h, w_ro_h, w_ei_h, w_eo_h, expert_of, slot_of, gate_prob, out,
    w_ri, w_ro, w_ei, w_eo, tok, normed, res_hid, rows_raw, out_rows, out_rows2, rows_near, rows_far,
    hid_near, hid, own_part, de_send, de_recv, e_keep, pair_send, pair_recv, xf_send, xf_recv, zf_send, zf_recv,
    dt_send, dt_recv, t_keep, xt_send, xt_recv, gate_col, id_col, w_sem, send_sem, recv_sem,
):
    count, width = tokens.shape
    cap = out_rows.shape[1]
    shards = tok.shape[0]
    me = lax.axis_index("mp")
    z = lax.axis_index("expert")
    core = lax.rem(me, 2)
    over = lax.rem(me + 2, 4)
    mate = me + 1 - 2 * core
    cross = lax.rem(mate + 2, 4)
    pair = z + 1 - 2 * lax.rem(z, 2)
    far = (lax.rem(z + 2, 4), 3 - z)
    to_over, to_mate, to_pair = {"mp": over}, {"mp": mate}, {"expert": pair}
    to_far = ({"expert": far[0]}, {"expert": far[1]})

    loads = []
    for k, (src, dst) in enumerate(((w_ri_h, w_ri), (w_ei_h.at[0], w_ei), (w_eo_h.at[0], w_eo), (w_ro_h, w_ro))):
        load = pltpu.make_async_copy(src, dst, w_sem.at[k])
        load.start()
        loads.append(load)

    barrier = pltpu.get_barrier_semaphore()
    for dest in (to_over, to_mate, to_pair, to_far[0], to_far[1]):
        pl.semaphore_signal(barrier, inc=1, device_id=dest, device_id_type=MESH)

    ids = jnp.where(slot_of[...] >= 0, expert_of[...] * cap + slot_of[...], -1).astype(F32)
    slot_rows = lax.broadcasted_iota(jnp.int32, (cap, count), 0).astype(F32)
    slot_cols = lax.broadcasted_iota(jnp.int32, (count, cap), 1).astype(F32)

    def send_table(e):
        base = (e * cap).astype(F32)
        return jnp.where(slot_rows + base == ids, 1.0, 0.0).astype(BF16)

    def take_table(e):
        base = (e * cap).astype(F32)
        return jnp.where(slot_cols + base == id_col[:, :1], 1.0, 0.0).astype(BF16)

    sent = []

    def send(src, dst, dest):
        k = len(sent)
        copy = pltpu.make_async_remote_copy(
            src_ref=src, dst_ref=dst, send_sem=send_sem.at[k], recv_sem=recv_sem.at[k],
            device_id=dest, device_id_type=MESH,
        )
        copy.start()
        sent.append(copy)
        return copy

    pl.semaphore_wait(barrier, 5)
    half = count // halves
    spans = [slice(h * half, (h + 1) * half) for h in range(halves)]
    tok_over = [send(tokens.at[r], tok.at[me, r], to_over) for r in spans]
    tok_mate = send(tokens, tok.at[me], to_mate)
    z_in = []
    for f in range(2):
        out_rows[f + 1] = dot(send_table(far[f]), tokens[...]).astype(BF16)
        z_in.append(send(out_rows.at[f + 1], rows_raw.at[me, f + 1], to_far[f]))
    pair_table = send_table(pair)
    out_rows[0] = dot(pair_table, tokens[...]).astype(BF16)
    pair_in = send(out_rows.at[0], rows_raw.at[me, 0], to_pair)
    tok[me] = tokens[...]
    id_col[...] = jnp.broadcast_to(ids, (128, count)).T
    gate_col[...] = jnp.broadcast_to(gate_prob[...], (128, count)).T

    def normalize(load, scale_rows, dst, lo):
        total = 0.0
        for s in range(shards):
            v = load(s).astype(F32)
            total = total + jnp.sum(v * v, axis=-1, keepdims=True)
        inverse = lax.rsqrt(total / (shards * width) + 1e-05)
        for s in range(shards):
            cols = slice(s * width, (s + 1) * width)
            dst[lo:lo + scale_rows, cols] = (load(s).astype(F32) * inverse * gain[:, cols]).astype(BF16)


    def shard_cols(s):
        return pl.ds(pl.multiple_of(s * width, width), width)

    tok_cross = []

    def relay(h):
        tok_over[h].wait_recv()
        piece = tok.at[over, spans[h]]
        tok_cross.append(send(piece, piece, to_mate))

    def residual(h):
        r = spans[h]
        tok_cross[h].wait_recv()
        normalize(lambda s: tok[s, r], half, normed, h * half)
        first_layer(normed, w_ri, res_hid, width, h * half, half)

    relay(0)
    tok_mate.wait_recv()
    loads[0].wait()
    for h in range(halves - 1):
        residual(h)
        relay(h + 1)
    out_rows2[...] = dot(pair_table, tok[over]).astype(BF16)
    pair_in2 = send(out_rows2, rows_raw.at[over, 0], to_pair)
    x_in, d_in = [], []
    for f in range(2):
        z_in[f].wait_recv()
        piece = rows_raw.at[me, f + 1]
        x_in.append(send(piece, piece, to_over))
        d_in.append(send(piece, piece, to_mate))
    residual(halves - 1)

    pair_in.wait_recv()
    pair_d = send(rows_raw.at[me, 0], rows_raw.at[me, 0], to_mate)
    pair_in2.wait_recv()
    pair_d2 = send(rows_raw.at[over, 0], rows_raw.at[over, 0], to_mate)
    rows_near[:cap, :] = dot(send_table(z), normed[...]).astype(BF16)
    pair_d.wait_recv()
    pair_d2.wait_recv()
    normalize(lambda s: rows_raw[s, 0], cap, rows_near, cap)
    loads[1].wait()
    first_layer(rows_near, w_ei, hid_near, width, 0, 2 * cap)

    d_in2 = []
    for f in range(2):
        x_in[f].wait_recv()
        piece = rows_raw.at[over, f + 1]
        d_in2.append(send(piece, piece, to_mate))
    loads[2].wait()
    de = {}
    for j, s in ((1, cross), (0, mate)):
        part = dot(hid_near[...], w_eo[:, shard_cols(s)])
        own_part[s] = part[:cap].astype(BF16)
        de_send[j, 0] = part[cap:].astype(BF16)
        de[j] = send(de_send.at[j, 0], de_recv.at[j, 0], to_mate)
    for j, s in ((1, over), (0, me)):
        part = dot(hid_near[...], w_eo[:, shard_cols(s)])
        own_part[s] = part[:cap].astype(BF16)
        e_keep[j, 0] = part[cap:]
    pair_out = {}
    for j in (1, 0):
        de[j].wait_recv()
        pair_send[j] = (e_keep[j, 0] + de_recv[j, 0].astype(F32)).astype(BF16)
        pair_out[j] = send(pair_send.at[j], pair_recv.at[j], to_pair)

    for f in range(2):
        d_in[f].wait_recv()
        d_in2[f].wait_recv()
        normalize(lambda s, f=f: rows_raw[s, f + 1], cap, rows_far, f * cap)
    first_layer(rows_far, w_ei, hid, width, 0, 2 * cap)
    de_far, xf = {}, []

    def far_give(j, s):
        part = dot(hid[...], w_eo[:, shard_cols(s)])
        for f in range(2):
            de_send[j, f + 1] = part[f * cap:(f + 1) * cap].astype(BF16)
            de_far[j, f] = send(de_send.at[j, f + 1], de_recv.at[j, f + 1], to_mate)

    def far_keep(j, s):
        part = dot(hid[...], w_eo[:, shard_cols(s)])
        for f in range(2):
            e_keep[j, f + 1] = part[f * cap:(f + 1) * cap]

    far_give(1, cross)
    far_keep(1, over)
    far_give(0, mate)
    for f in range(2):
        de_far[1, f].wait_recv()
        xf_send[f] = (e_keep[1, f + 1] + de_recv[1, f + 1].astype(F32)).astype(BF16)
        xf.append(send(xf_send.at[f], xf_recv.at[f], to_over))
    far_keep(0, me)

    loads[3].wait()
    own_take = take_table(z)
    pair_take = take_table(pair)
    dt = {}

    def token_part(s):
        return dot(res_hid[...], w_ro[:, shard_cols(s)]) + gate_col[:, :1] * dot(own_take, own_part[s])

    def token_give(j, s):
        dt_send[j] = token_part(s).astype(BF16)
        dt[j] = send(dt_send.at[j], dt_recv.at[j], to_mate)

    def chip_sum(j):
        pair_out[j].wait_recv()
        dt[j].wait_recv()
        return t_keep[j] + dt_recv[j].astype(F32) + gate_col[:, :1] * dot(pair_take, pair_recv[j])

    zf = []

    def far_home(f):
        xf[f].wait_recv()
        de_far[0, f].wait_recv()
        full = e_keep[0, f + 1] + de_recv[0, f + 1].astype(F32) + xf_recv[f].astype(F32)
        zf_send[f] = full.astype(BF16)
        zf.append(send(zf_send.at[f], zf_recv.at[f], to_far[f]))

    token_give(1, cross)
    t_keep[1] = token_part(over)
    far_home(0)
    xt_send[...] = chip_sum(1).astype(BF16)
    xt = send(xt_send, xt_recv, to_over)
    far_home(1)
    token_give(0, mate)
    t_keep[0] = token_part(me)
    t_keep[0] = chip_sum(0)
    for f in range(2):
        far_take = take_table(far[f])
        zf[f].wait_recv()
        t_keep[0] = t_keep[0] + gate_col[:, :1] * dot(far_take, zf_recv[f])
    xt.wait_recv()
    out[...] = (t_keep[0] + xt_recv[...].astype(F32)).astype(BF16)
    for copy in sent:
        copy.wait_send()


def fused(tokens, gain, w_res_in, w_res_out, w_exp_in, w_exp_out, expert_of, slot_of, gate_prob):
    count, width = tokens.shape
    shards = lax.axis_size("mp")
    experts = lax.axis_size("expert")
    cap = max(2, 5 * count // (4 * experts))
    model, hidden = w_res_in.shape
    exp_hidden = w_exp_in.shape[2]
    vmem, hbm = pl.BlockSpec(memory_space=pltpu.VMEM), pl.BlockSpec(memory_space=pl.ANY)
    buf = lambda *shape: pltpu.VMEM(shape, BF16)
    wide = lambda *shape: pltpu.VMEM(shape, F32)
    halves = 2
    copies = 28 + 2 * halves
    return pl.pallas_call(
        functools.partial(fused_kernel, halves),
        out_shape=jax.ShapeDtypeStruct((count, width), BF16),
        in_specs=[vmem, vmem, hbm, hbm, hbm, hbm, vmem, vmem, vmem],
        out_specs=vmem,
        scratch_shapes=[
            buf(model, hidden), buf(hidden, model), buf(model, exp_hidden), buf(exp_hidden, model),
            buf(shards, count, width), buf(count, model), buf(count, hidden),
            buf(shards, 3, cap, width), buf(3, cap, width), buf(cap, width),
            buf(2 * cap, model), buf(2 * cap, model), buf(2 * cap, exp_hidden), buf(2 * cap, exp_hidden),
            buf(shards, cap, width), buf(2, 3, cap, width), buf(2, 3, cap, width), wide(2, 3, cap, width),
            buf(2, cap, width), buf(2, cap, width), buf(2, cap, width), buf(2, cap, width),
            buf(2, cap, width), buf(2, cap, width),
            buf(2, count, width), buf(2, count, width), wide(2, count, width),
            buf(count, width), buf(count, width), wide(count, 128), wide(count, 128),
            pltpu.SemaphoreType.DMA((4,)), pltpu.SemaphoreType.DMA((copies,)), pltpu.SemaphoreType.DMA((copies,)),
        ],
        name="fused_layer",
        compiler_params=pltpu.CompilerParams(
            collective_id=0, has_side_effects=True, vmem_limit_bytes=56 * 1024 * 1024
        ),
    )(
        tokens, gain[None, :], w_res_in, w_res_out, w_exp_in, w_exp_out,
        expert_of[None, :], slot_of[None, :], gate_prob[None, :],
    )


def pick(mesh):
    if mesh.shape["mp"] == 4 and mesh.shape["expert"] == 4:
        return fused
    return per_device


def solution(mesh):
    return jax.shard_map(
        pick(mesh),
        mesh=mesh,
        in_specs=(
            P(("groups", "expert"), "mp"),
            P(),
            P(None, "mp"),
            P("mp", None),
            P("expert", None, "mp"),
            P("expert", "mp", None),
            P(("groups", "expert")),
            P(("groups", "expert")),
            P(("groups", "expert")),
        ),
        out_specs=P(("groups", "expert"), "mp"),
        check_vma=False,
    )
```

profile of v0, /device:TPU:0, one launch (start us, length us, event | category | flops | bytes accessed | tf_op | source)
XLA Modules:
  0.0 53.7 jit_solution(5149694623706680710)
XLA Ops:
  0.0 1.3 %broadcast_in_dim.13.expert_of = s32[1,768]{1,0:T(1,128)} reshape(s32[768]{0:T(1024)} %param.15) | data formatting | bytes 6144 | tf_op jit(solution)/shard_map/broadcast_in_dim | solution.py:344
  1.3 1.3 %broadcast_in_dim.14.slot_of = s32[1,768]{1,0:T(1,128)} reshape(s32[768]{0:T(1024)} %param.16) | data formatting | bytes 6144 | tf_op jit(solution)/shard_map/broadcast_in_dim | solution.py:344
  2.5 1.3 %broadcast_in_dim.15.gate_prob = f32[1,768]{1,0:T(1,128)} reshape(f32[768]{0:T(1024)} %param.17) | data formatting | bytes 6144 | tf_op jit(solution)/shard_map/broadcast_in_dim | solution.py:344
  3.8 48.1 %fused_layer.1 = bf16[768,256]{1,0:T(8,128)(2,1)} custom-call(bf16[768,256]{1,0:T(8,128)(2,1)} %tokens.1, f32[1,1024]{1,0:T(1,128)} %bitcast.1, bf16[1024,1024]{1,0:T(8,128)(2,1)} %w_ri_h.1, bf16[1024,1024]{1,0:T(8,128)(2,1)} %w_ro_h.1, bf16[1,1024,1024]{2,1,0:T(8,128)(2,1)} %w_ei_h.1, bf16[1,1024,1024]{2,1,0:T(8,128)(2,1)} %w_eo_h.1, ...), custom_call_target="tpu_custom_call" | custom-call | tf_op jit(solution)/shard_map/fused_layer/pallas_call | solution.py:321
  52.0 1.8 %copy.11 = bf16[768,256]{1,0:T(8,128)(2,1)} copy(bf16[768,256]{1,0:T(8,128)(2,1)} %fused_layer.1) | data formatting | bytes 786432
where the time goes:
time: 54 us; the launch traced here: 53.7 us
  Pallas kernels  48.1 us (89%)
  local copies, waits for them, and re-layouts  5.57 us (10%)
    pallas_call x1, Pallas kernels, fused(): pl.pallas_call(functools.partial(fused_kernel, halves), out_shape=jax.Sha...  48.1 us
    unnamed x1, local copies, waits for them, and re-layouts  1.77 us
    broadcast_in_dim x1, local copies, waits for them, and re-layouts, fused(): gate_prob[None, :]  1.28 us
    broadcast_in_dim x1, local copies, waits for them, and re-layouts, fused(): expert_of[None, :]  1.27 us
    broadcast_in_dim x1, local copies, waits for them, and re-layouts, fused(): slot_of[None, :]  1.27 us

commit v1 on v0

v1 whole, which is shorter than its diff:
```python
import functools

import jax
import jax.numpy as jnp
from jax import lax
from jax.experimental import pallas as pl
from jax.experimental.pallas import tpu as pltpu
from jax.sharding import PartitionSpec as P


def rms_rows(tokens, gain):
    values = tokens.astype(jnp.float32)
    inverse = lax.rsqrt(jnp.mean(values * values, axis=-1, keepdims=True) + 1e-05)
    return (values * inverse * gain).astype(jnp.bfloat16)


def per_device(
    tokens, gain, w_res_in, w_res_out, w_exp_in, w_exp_out, expert_of, slot_of, gate_prob
):
    full_rows = lax.all_gather(tokens, "mp", axis=1, tiled=True)
    normed = rms_rows(full_rows, gain)
    res_hidden = jax.nn.gelu(jnp.dot(normed, w_res_in, preferred_element_type=jnp.float32)).astype(
        jnp.bfloat16
    )
    res_part = jnp.dot(res_hidden, w_res_out, preferred_element_type=jnp.float32)
    row_count = expert_of.shape[0]
    experts = lax.axis_size("expert")
    capacity = max(2, 5 * row_count // (4 * experts))
    feat_width = tokens.shape[1]
    slot_id = jnp.where(slot_of >= 0, expert_of * capacity + slot_of, -1)
    slot_index = jnp.arange(experts * capacity, dtype=jnp.int32)
    send_table = (slot_index[:, None] == slot_id[None, :]).astype(jnp.bfloat16)
    take_table = (slot_id[:, None] == slot_index[None, :]).astype(jnp.bfloat16)
    local_in = w_exp_in[0]
    local_out = w_exp_out[0]
    mp_index = lax.axis_index("mp")
    own_slice = lax.dynamic_slice_in_dim(normed, mp_index * feat_width, feat_width, 1)
    outgoing = jnp.dot(send_table, own_slice, preferred_element_type=jnp.float32).astype(
        jnp.bfloat16
    )
    incoming = lax.all_to_all(
        outgoing.reshape(experts, capacity, feat_width),
        "expert",
        split_axis=0,
        concat_axis=0,
        tiled=True,
    )
    piece = lax.all_gather(incoming, "mp", axis=2, tiled=True)
    flat_piece = piece.reshape(-1, piece.shape[2])
    preact = jnp.dot(flat_piece, local_in, preferred_element_type=jnp.float32)
    exp_hidden = jax.nn.gelu(preact).astype(jnp.bfloat16)
    exp_part = jnp.dot(exp_hidden, local_out, preferred_element_type=jnp.float32)
    gate_column = gate_prob[:, None]
    summed = lax.psum_scatter(exp_part.astype(jnp.bfloat16), "mp", scatter_dimension=1, tiled=True)
    returned = lax.all_to_all(
        summed.reshape(experts, capacity, feat_width),
        "expert",
        split_axis=0,
        concat_axis=0,
        tiled=True,
    )
    moe_value = jnp.dot(
        take_table,
        returned.reshape(experts * capacity, feat_width),
        preferred_element_type=jnp.float32,
    )
    res_sum = lax.psum_scatter(
        res_part.astype(jnp.bfloat16), "mp", scatter_dimension=1, tiled=True
    ).astype(jnp.float32)
    return (res_sum + gate_column * moe_value).astype(jnp.bfloat16)


MESH = pl.DeviceIdType.MESH
F32 = jnp.float32
BF16 = jnp.bfloat16


def dot(a, b):
    return jnp.dot(a, b, preferred_element_type=F32)


def gelu_rows(rows, w_ref):
    return jax.nn.gelu(dot(rows, w_ref[...])).astype(BF16)


def fused_kernel(
    spans, pieces, tokens_h, gain_h, w_ri_h, w_ro_h, w_ei_h, w_eo_h, expert_h, slot_h, gate_h, out,
    expert_v, slot_v, gate_v, gain, w_ri, w_ro, w_ei, w_eo, tok, normed, res_hid, rows_raw, out_rows, out_rows2,
    rows_near, rows_far, hid_near, hid, own_part, de_send, de_recv, e_keep, pair_send, pair_recv, xf_send, xf_recv,
    zf_send, zf_recv, dt_send, dt_recv, t_keep, xt_send, xt_recv, gate_col, id_col, load_sem, send_sem, recv_sem,
):
    shards, count, width = tok.shape
    cap = out_rows.shape[1]
    me = lax.axis_index("mp")
    z = lax.axis_index("expert")
    core = lax.rem(me, 2)
    over = lax.rem(me + 2, 4)
    mate = me + 1 - 2 * core
    cross = lax.rem(mate + 2, 4)
    pair = z + 1 - 2 * lax.rem(z, 2)
    far = (lax.rem(z + 2, 4), 3 - z)
    to_over, to_mate, to_pair = {"mp": over}, {"mp": mate}, {"expert": pair}
    to_far = ({"expert": far[0]}, {"expert": far[1]})

    barrier = pltpu.get_barrier_semaphore()
    for dest in (to_over, to_mate, to_pair, to_far[0], to_far[1]):
        pl.semaphore_signal(barrier, inc=1, device_id=dest, device_id_type=MESH)

    loads = []
    for k, (src, dst) in enumerate((
        (expert_h, expert_v), (slot_h, slot_v), (tokens_h, tok.at[me]), (gate_h, gate_v), (gain_h, gain),
        (w_ri_h, w_ri), (w_ei_h.at[0], w_ei), (w_eo_h.at[0], w_eo), (w_ro_h, w_ro),
    )):
        load = pltpu.make_async_copy(src, dst, load_sem.at[k])
        load.start()
        loads.append(load)

    sent = []

    def send(src, dst, dest):
        k = len(sent)
        copy = pltpu.make_async_remote_copy(
            src_ref=src, dst_ref=dst, send_sem=send_sem.at[k], recv_sem=recv_sem.at[k],
            device_id=dest, device_id_type=MESH,
        )
        copy.start()
        sent.append(copy)
        return copy

    def pass_on(ref, dest):
        return send(ref, ref, dest)

    def send_table(e):
        base = (e * cap).astype(F32)
        return jnp.where(slot_rows + base == ids, 1.0, 0.0).astype(BF16)

    def take_table(e):
        base = (e * cap).astype(F32)
        return jnp.where(slot_cols + base == id_col[:, :1], 1.0, 0.0).astype(BF16)

    def shard_cols(s):
        return pl.ds(pl.multiple_of(s * width, width), width)

    def normalize(load, dst, rows):
        total = 0.0
        for s in range(shards):
            v = load(s).astype(F32)
            total = total + jnp.sum(v * v, axis=-1, keepdims=True)
        inverse = lax.rsqrt(total / (shards * width) + 1e-05)
        for s in range(shards):
            cols = slice(s * width, (s + 1) * width)
            dst[rows, cols] = (load(s).astype(F32) * inverse * gain[:, cols]).astype(BF16)

    with jax.named_scope("entry"):
        loads[0].wait()
        loads[1].wait()
        expert_row = expert_v[...].reshape(1, count)
        slot_row = slot_v[...].reshape(1, count)
        ids = jnp.where(slot_row >= 0, expert_row * cap + slot_row, -1).astype(F32)
        slot_rows = lax.broadcasted_iota(jnp.int32, (cap, count), 0).astype(F32)
        slot_cols = lax.broadcasted_iota(jnp.int32, (count, cap), 1).astype(F32)
        loads[2].wait()
        for k, e in enumerate((pair, far[0], far[1])):
            out_rows[k] = dot(send_table(e), tok[me]).astype(BF16)
    with jax.named_scope("barrier"):
        pl.semaphore_wait(barrier, 5)

    tok_over = [send(tok.at[me, r], tok.at[me, r], to_over) for r in spans]
    tok_mate = pass_on(tok.at[me], to_mate)
    z_in = [None, None]

    def far_send(f):
        z_in[f] = [send(out_rows.at[f + 1, r], rows_raw.at[me, f + 1, r], to_far[f]) for r in pieces]

    far_send(0)
    pair_in = send(out_rows.at[0], rows_raw.at[me, 0], to_pair)
    far_send(1)
    with jax.named_scope("columns"):
        id_col[...] = jnp.broadcast_to(ids, (128, count)).T
        loads[3].wait()
        gate_col[...] = jnp.broadcast_to(gate_v[...].reshape(1, count), (128, count)).T
        for k in range(4, 9):
            loads[k].wait()

    tok_cross = []

    def relay(h):
        with jax.named_scope(f"relay{h}"):
            tok_over[h].wait_recv()
            tok_cross.append(pass_on(tok.at[over, spans[h]], to_mate))

    def residual(h):
        r = spans[h]
        with jax.named_scope(f"reswait{h}"):
            tok_cross[h].wait_recv()
        with jax.named_scope(f"residual{h}"):
            normalize(lambda s: tok[s, r], normed, r)
            res_hid[r] = gelu_rows(normed[r], w_ri)

    x_in, d_in, d_in2 = ([], []), ([], []), ([], [])

    def far_in(f, p):
        with jax.named_scope(f"farin{f}{p}"):
            z_in[f][p].wait_recv()
            piece = rows_raw.at[me, f + 1, pieces[p]]
            x_in[f].append(pass_on(piece, to_over))
            d_in[f].append(pass_on(piece, to_mate))

    def far_cross(f, p):
        with jax.named_scope(f"farcross{f}{p}"):
            x_in[f][p].wait_recv()
            d_in2[f].append(pass_on(rows_raw.at[over, f + 1, pieces[p]], to_mate))

    de = {}

    def give(e, j, s, hid_ref):
        de_send[j, e] = dot(hid_ref[...], w_eo[:, shard_cols(s)]).astype(BF16)
        de[j, e] = send(de_send.at[j, e], de_recv.at[j, e], to_mate)

    def keep(e, j, s, hid_ref):
        e_keep[j, e] = dot(hid_ref[...], w_eo[:, shard_cols(s)])

    def chip_part(e, j):
        de[j, e].wait_recv()
        return e_keep[j, e] + de_recv[j, e].astype(F32)

    def expert_rows(e, hid_ref):
        with jax.named_scope(f"expert{e}"):
            normalize(lambda s: rows_raw[s, e], rows_far.at[e], slice(0, cap))
            hid_ref[...] = gelu_rows(rows_far[e], w_ei)
            give(e, 1, cross, hid_ref)
            keep(e, 1, over, hid_ref)
            give(e, 0, mate, hid_ref)
            keep(e, 0, me, hid_ref)

    last = len(pieces)
    relay(0)
    tok_mate.wait_recv()
    residual(0)
    for p in range(last):
        far_in(0, p)
    for h in range(1, len(spans)):
        relay(h)
    with jax.named_scope("pairsend"):
        out_rows2[...] = dot(send_table(pair), tok[over]).astype(BF16)
        pair_in2 = send(out_rows2, rows_raw.at[over, 0], to_pair)
    for p in range(last - 1):
        far_in(1, p)
    for h in range(1, len(spans)):
        residual(h)
    far_in(1, last - 1)
    for p in range(last):
        far_cross(0, p)
    with jax.named_scope("ownfirst"):
        rows_near[...] = dot(send_table(z), normed[...]).astype(BF16)
        hid_near[...] = gelu_rows(rows_near[...], w_ei)
    with jax.named_scope("farwait0"):
        for p in range(last):
            d_in[0][p].wait_recv()
            d_in2[0][p].wait_recv()
    expert_rows(1, hid.at[1])
    with jax.named_scope("pairrelay"):
        pair_in.wait_recv()
        pair_d = pass_on(rows_raw.at[me, 0], to_mate)
        pair_in2.wait_recv()
        pair_d2 = pass_on(rows_raw.at[over, 0], to_mate)
    for p in range(last):
        far_cross(1, p)
    xf, zf = [], []

    def far_out(f):
        with jax.named_scope(f"farout{f}"):
            xf_send[f] = chip_part(f + 1, 1).astype(BF16)
            xf.append(send(xf_send.at[f], xf_recv.at[f], to_over))

    def far_home(f):
        with jax.named_scope(f"farhome{f}"):
            xf[f].wait_recv()
            zf_send[f] = (chip_part(f + 1, 0) + xf_recv[f].astype(F32)).astype(BF16)
            zf.append(send(zf_send.at[f], zf_recv.at[f], to_far[f]))

    pair_out = {}

    def pair_home(j):
        with jax.named_scope(f"pairhome{j}"):
            pair_send[j] = chip_part(0, j).astype(BF16)
            pair_out[j] = send(pair_send.at[j], pair_recv.at[j], to_pair)

    far_out(0)
    with jax.named_scope("pairwait"):
        pair_d.wait_recv()
        pair_d2.wait_recv()
    expert_rows(0, hid.at[0])
    with jax.named_scope("farwait1"):
        for p in range(last):
            d_in[1][p].wait_recv()
            d_in2[1][p].wait_recv()
    expert_rows(2, hid.at[2])
    pair_home(1)
    far_out(1)
    far_home(0)
    pair_home(0)
    with jax.named_scope("ownsecond"):
        for s in range(shards):
            own_part[s] = dot(hid_near[...], w_eo[:, s * width:(s + 1) * width]).astype(BF16)
        own_take = take_table(z)
        pair_take = take_table(pair)
    dt = {}

    def token_part(s):
        return dot(res_hid[...], w_ro[:, shard_cols(s)]) + gate_col[:, :1] * dot(own_take, own_part[s])

    def token_give(j, s):
        dt_send[j] = token_part(s).astype(BF16)
        dt[j] = send(dt_send.at[j], dt_recv.at[j], to_mate)

    def chip_sum(j):
        pair_out[j].wait_recv()
        dt[j].wait_recv()
        return t_keep[j] + dt_recv[j].astype(F32) + gate_col[:, :1] * dot(pair_take, pair_recv[j])

    with jax.named_scope("tokens1"):
        token_give(1, cross)
        t_keep[1] = token_part(over)
    with jax.named_scope("tokensend"):
        xt_send[...] = chip_sum(1).astype(BF16)
        xt = send(xt_send, xt_recv, to_over)
    with jax.named_scope("tokens0"):
        token_give(0, mate)
        t_keep[0] = token_part(me)
    far_home(1)
    with jax.named_scope("tokenkeep"):
        t_keep[0] = chip_sum(0)
    for f in range(2):
        with jax.named_scope(f"fartake{f}"):
            far_take = take_table(far[f])
            zf[f].wait_recv()
            t_keep[0] = t_keep[0] + gate_col[:, :1] * dot(far_take, zf_recv[f])
    with jax.named_scope("final"):
        xt.wait_recv()
        out[...] = (t_keep[0] + xt_recv[...].astype(F32)).astype(BF16)
        for copy in sent:
            copy.wait_send()


def split_rows(rows, parts):
    step = -(-rows // (16 * parts)) * 16
    return tuple(slice(lo, min(lo + step, rows)) for lo in range(0, rows, step))


def fused(tokens, gain, w_res_in, w_res_out, w_exp_in, w_exp_out, expert_of, slot_of, gate_prob):
    count, width = tokens.shape
    shards = lax.axis_size("mp")
    experts = lax.axis_size("expert")
    cap = max(2, 5 * count // (4 * experts))
    model, hidden = w_res_in.shape
    exp_hidden = w_exp_in.shape[2]
    vmem, hbm = pl.BlockSpec(memory_space=pltpu.VMEM), pl.BlockSpec(memory_space=pltpu.HBM)
    buf = lambda *shape: pltpu.VMEM(shape, BF16)
    wide = lambda *shape: pltpu.VMEM(shape, F32)
    spans, pieces = split_rows(count, 2), split_rows(cap, 2)
    copies = 20 + 2 * len(spans) + 8 * len(pieces)
    args = (
        tokens, gain[None, :], w_res_in, w_res_out, w_exp_in, w_exp_out, expert_of, slot_of, gate_prob,
    )
    return pl.pallas_call(
        functools.partial(fused_kernel, spans, pieces),
        out_shape=jax.ShapeDtypeStruct((count, width), BF16),
        in_specs=[hbm] * len(args),
        out_specs=vmem,
        scratch_shapes=[
            pltpu.VMEM((count,), jnp.int32), pltpu.VMEM((count,), jnp.int32), wide(count), wide(1, model),
            buf(model, hidden), buf(hidden, model), buf(model, exp_hidden), buf(exp_hidden, model),
            buf(shards, count, width), buf(count, model), buf(count, hidden),
            buf(shards, 3, cap, width), buf(3, cap, width), buf(cap, width),
            buf(cap, model), buf(3, cap, model), buf(cap, exp_hidden), buf(3, cap, exp_hidden),
            buf(shards, cap, width), buf(2, 3, cap, width), buf(2, 3, cap, width), wide(2, 3, cap, width),
            buf(2, cap, width), buf(2, cap, width), buf(2, cap, width), buf(2, cap, width),
            buf(2, cap, width), buf(2, cap, width),
            buf(2, count, width), buf(2, count, width), wide(2, count, width),
            buf(count, width), buf(count, width), wide(count, 128), wide(count, 128),
            pltpu.SemaphoreType.DMA((9,)), pltpu.SemaphoreType.DMA((copies,)), pltpu.SemaphoreType.DMA((copies,)),
        ],
        name="fused_layer",
        compiler_params=pltpu.CompilerParams(
            collective_id=0, has_side_effects=True, vmem_limit_bytes=50 * 1024 * 1024
        ),
    )(*(pltpu.with_memory_space_constraint(a, pltpu.HBM) for a in args))


def pick(mesh):
    if mesh.shape["mp"] == 4 and mesh.shape["expert"] == 4:
        return fused
    return per_device


def solution(mesh):
    return jax.shard_map(
        pick(mesh),
        mesh=mesh,
        in_specs=(
            P(("groups", "expert"), "mp"),
            P(),
            P(None, "mp"),
            P("mp", None),
            P("expert", None, "mp"),
            P("expert", "mp", None),
            P(("groups", "expert")),
            P(("groups", "expert")),
            P(("groups", "expert")),
        ),
        out_specs=P(("groups", "expert"), "mp"),
        check_vma=False,
    )
```

time: 54 us -> 46.8 us (0.87)
  local copies, waits for them, and re-layouts: 5.57 us -> 0.75 us
  Pallas kernels: 48.1 us -> 45.8 us
    broadcast_in_dim x3 -> x0, local copies, waits for them, and re-layouts: 3.81 us -> none  [the longest x1 1.28 us: fused(): gate_prob[None, :]]
    pallas_call x1, Pallas kernels: 48.1 us -> 45.8 us  [fused(): pl.pallas_call(functools.partial(fused_kernel, spans, pieces), out_shape=...]
    unnamed x1, local copies, waits for them, and re-layouts: 1.77 us -> 0.75 us
where the time goes in v1:
time: 46.8 us; the launch traced here: 46.6 us
  Pallas kernels  45.8 us (98%)
  local copies, waits for them, and re-layouts  0.75 us (2%)
    pallas_call x1, Pallas kernels, fused(): pl.pallas_call(functools.partial(fused_kernel, spans, pieces), out_shape=...  45.8 us

profile of v1, /device:TPU:0, one launch (start us, length us, event | category | flops | bytes accessed | tf_op | source)
XLA Modules:
  0.0 46.6 jit_solution(6734876255699007246)
XLA Ops:
  0.0 45.8 %fused_layer.1 = bf16[768,256]{1,0:T(8,128)(2,1)S(1)} custom-call(bf16[768,256]{1,0:T(8,128)(2,1)} %tokens_h.1, f32[1,1024]{1,0:T(1,128)} %bitcast.1, bf16[1024,1024]{1,0:T(8,128)(2,1)} %w_ri_h.1, bf16[1024,1024]{1,0:T(8,128)(2,1)} %w_ro_h.1, bf16[1,1024,1024]{2,1,0:T(8,128)(2,1)} %w_ei_h.1, bf16[1,1024,1024]{2,1,0:T(8,128)(2,1)} %w_eo_h.1, s32[768]{0:T(1024)} %expert_h.1, ...), custom_call_target="tpu_custom_call" | custom-call | tf_op jit(solution)/shard_map/fused_layer/pallas_call | solution.py:366
  45.8 0.7 %copy.11 = bf16[768,256]{1,0:T(8,128)(2,1)} copy(bf16[768,256]{1,0:T(8,128)(2,1)S(1)} %fused_layer.1) | data formatting | bytes 786432

commit v2 on v1

v2 whole, which is shorter than its diff:
```python
import functools

import jax
import jax.numpy as jnp
from jax import lax
from jax.experimental import pallas as pl
from jax.experimental.pallas import tpu as pltpu
from jax.sharding import PartitionSpec as P


def rms_rows(tokens, gain):
    values = tokens.astype(jnp.float32)
    inverse = lax.rsqrt(jnp.mean(values * values, axis=-1, keepdims=True) + 1e-05)
    return (values * inverse * gain).astype(jnp.bfloat16)


def per_device(
    tokens, gain, w_res_in, w_res_out, w_exp_in, w_exp_out, expert_of, slot_of, gate_prob
):
    full_rows = lax.all_gather(tokens, "mp", axis=1, tiled=True)
    normed = rms_rows(full_rows, gain)
    res_hidden = jax.nn.gelu(jnp.dot(normed, w_res_in, preferred_element_type=jnp.float32)).astype(
        jnp.bfloat16
    )
    res_part = jnp.dot(res_hidden, w_res_out, preferred_element_type=jnp.float32)
    row_count = expert_of.shape[0]
    experts = lax.axis_size("expert")
    capacity = max(2, 5 * row_count // (4 * experts))
    feat_width = tokens.shape[1]
    slot_id = jnp.where(slot_of >= 0, expert_of * capacity + slot_of, -1)
    slot_index = jnp.arange(experts * capacity, dtype=jnp.int32)
    send_table = (slot_index[:, None] == slot_id[None, :]).astype(jnp.bfloat16)
    take_table = (slot_id[:, None] == slot_index[None, :]).astype(jnp.bfloat16)
    local_in = w_exp_in[0]
    local_out = w_exp_out[0]
    mp_index = lax.axis_index("mp")
    own_slice = lax.dynamic_slice_in_dim(normed, mp_index * feat_width, feat_width, 1)
    outgoing = jnp.dot(send_table, own_slice, preferred_element_type=jnp.float32).astype(
        jnp.bfloat16
    )
    incoming = lax.all_to_all(
        outgoing.reshape(experts, capacity, feat_width),
        "expert",
        split_axis=0,
        concat_axis=0,
        tiled=True,
    )
    piece = lax.all_gather(incoming, "mp", axis=2, tiled=True)
    flat_piece = piece.reshape(-1, piece.shape[2])
    preact = jnp.dot(flat_piece, local_in, preferred_element_type=jnp.float32)
    exp_hidden = jax.nn.gelu(preact).astype(jnp.bfloat16)
    exp_part = jnp.dot(exp_hidden, local_out, preferred_element_type=jnp.float32)
    gate_column = gate_prob[:, None]
    summed = lax.psum_scatter(exp_part.astype(jnp.bfloat16), "mp", scatter_dimension=1, tiled=True)
    returned = lax.all_to_all(
        summed.reshape(experts, capacity, feat_width),
        "expert",
        split_axis=0,
        concat_axis=0,
        tiled=True,
    )
    moe_value = jnp.dot(
        take_table,
        returned.reshape(experts * capacity, feat_width),
        preferred_element_type=jnp.float32,
    )
    res_sum = lax.psum_scatter(
        res_part.astype(jnp.bfloat16), "mp", scatter_dimension=1, tiled=True
    ).astype(jnp.float32)
    return (res_sum + gate_column * moe_value).astype(jnp.bfloat16)


MESH = pl.DeviceIdType.MESH
F32 = jnp.float32
BF16 = jnp.bfloat16


def dot(a, b):
    return jnp.dot(a, b, preferred_element_type=F32)


def twice_gelu(x):
    bent = x * (0.7978845608028654 + 0.035677408136300125 * (x * x))
    return (x + x * jnp.tanh(bent)).astype(BF16)


def fused_kernel(
    spans, pieces, cap, tokens_h, gain_h, w_ri_h, w_ro_h, w_ei_h, w_eo_h, expert_h, slot_h, gate_h, out,
    expert_v, slot_v, gate_v, gain, w_ri, w_ro, w_ei, w_eo, tok, normed, res_hid, rows_raw, out_rows, out_rows2,
    rows_own, hid_own, rows_far, hid, part, de_recv, pair_send, pair_recv, xf_send, xf_recv, zf_send, zf_recv,
    back, take, slot_gate, tpart, dt_recv, t_keep, xt_send, xt_recv, id_col, load_sem, send_sem, recv_sem,
):
    shards, count, width = tok.shape
    padded = take.shape[2]
    hidden = res_hid.shape[1] - padded
    me = lax.axis_index("mp")
    z = lax.axis_index("expert")
    core = lax.rem(me, 2)
    chip = me // 2
    over = lax.rem(me + 2, 4)
    mate = me + 1 - 2 * core
    cross = lax.rem(mate + 2, 4)
    pair = z + 1 - 2 * lax.rem(z, 2)
    far = (lax.rem(z + 2, 4), 3 - z)
    to_over, to_mate, to_pair = {"mp": over}, {"mp": mate}, {"expert": pair}
    to_far = ({"expert": far[0]}, {"expert": far[1]})

    barrier = pltpu.get_barrier_semaphore()
    for dest in (to_over, to_mate, to_pair, to_far[0], to_far[1]):
        pl.semaphore_signal(barrier, inc=1, device_id=dest, device_id_type=MESH)

    loads = []
    for k, (src, dst) in enumerate((
        (expert_h, expert_v), (slot_h, slot_v), (tokens_h, tok.at[me]), (gate_h, gate_v), (gain_h, gain),
        (w_ri_h, w_ri), (w_ei_h.at[0], w_ei), (w_eo_h.at[0], w_eo), (w_ro_h, w_ro.at[:hidden]),
    )):
        load = pltpu.make_async_copy(src, dst, load_sem.at[k])
        load.start()
        loads.append(load)

    sent = []

    def send(src, dst, dest):
        k = len(sent)
        copy = pltpu.make_async_remote_copy(
            src_ref=src, dst_ref=dst, send_sem=send_sem.at[k], recv_sem=recv_sem.at[k],
            device_id=dest, device_id_type=MESH,
        )
        copy.start()
        sent.append(copy)
        return copy

    def pass_on(ref, dest):
        return send(ref, ref, dest)

    def send_table(e):
        base = (e * cap).astype(F32)
        return jnp.where(slot_rows + base == ids, 1.0, 0.0).astype(BF16)

    def chip_cols(j):
        block = chip if j == 0 else 1 - chip
        return pl.ds(pl.multiple_of(block * 2 * width, 2 * width), 2 * width)

    def normalize(load, dst, rows):
        total = 0.0
        for s in range(shards):
            v = load(s).astype(F32)
            total = total + jnp.sum(v * v, axis=-1, keepdims=True)
        inverse = lax.rsqrt(total / (shards * width) + 1e-05)
        for s in range(shards):
            cols = slice(s * width, (s + 1) * width)
            dst[rows, cols] = (load(s).astype(F32) * inverse * gain[:, cols]).astype(BF16)

    z_in = [None, None]

    def far_send(f):
        out_rows[f + 1] = dot(send_table(far[f]), tok[me]).astype(BF16)
        z_in[f] = [send(out_rows.at[f + 1, r], rows_raw.at[me, f + 1, r], to_far[f]) for r in pieces]

    with jax.named_scope("entry"):
        loads[0].wait()
        loads[1].wait()
        expert_row = expert_v[...].reshape(1, count)
        slot_row = slot_v[...].reshape(1, count)
        ids = jnp.where(slot_row >= 0, expert_row * cap + slot_row, -1).astype(F32)
        slot_rows = lax.broadcasted_iota(jnp.int32, (cap, count), 0).astype(F32)
        loads[2].wait()
    with jax.named_scope("barrier"):
        pl.semaphore_wait(barrier, 5)
    with jax.named_scope("dispatch"):
        tok_over = [pass_on(tok.at[me, r], to_over) for r in spans]
        tok_mate = pass_on(tok.at[me], to_mate)
        far_send(0)
        out_rows[0] = dot(send_table(pair), tok[me]).astype(BF16)
        pair_in = send(out_rows.at[0], rows_raw.at[me, 0], to_pair)
        far_send(1)
    with jax.named_scope("columns"):
        loads[3].wait()
        gate_row = gate_v[...].reshape(1, count)
        id_col[...] = jnp.broadcast_to(ids, (128, count)).T
        lanes = lax.broadcasted_iota(jnp.int32, (count, 128), 1).astype(F32)
        for k, e in enumerate((pair, far[0], far[1], z)):
            base = (e * cap).astype(F32)
            gates = jnp.sum(jnp.where(slot_rows + base == ids, gate_row, 0.0), axis=1, keepdims=True)
            slot_gate[k] = jnp.broadcast_to(gates, (cap, 128))
            for lo in range(0, padded, 128):
                hit = jnp.where(lanes + (base + lo) == id_col[...], 1.0, 0.0).astype(BF16)
                if k < 3:
                    take[k, :, lo:lo + 128] = hit
                else:
                    res_hid[:, hidden + lo:hidden + lo + 128] = hit
        back[:, cap:, :] = jnp.zeros((4, padded - cap, width), BF16)
        for k in range(4, 9):
            loads[k].wait()
        w_ro[hidden + cap:, :] = jnp.zeros((padded - cap, shards * width), BF16)

    def gated(rows, k):
        scale = slot_gate[k]
        return (rows * jnp.concatenate([scale] * (rows.shape[1] // 128), axis=1)).astype(BF16)

    tok_cross = []

    def relay(h):
        with jax.named_scope(f"relay{h}"):
            tok_over[h].wait_recv()
            tok_cross.append(pass_on(tok.at[over, spans[h]], to_mate))

    def residual(h):
        r = spans[h]
        with jax.named_scope(f"reswait{h}"):
            tok_cross[h].wait_recv()
        with jax.named_scope(f"residual{h}"):
            normalize(lambda s: tok[s, r], normed, r)
            res_hid[r, :hidden] = twice_gelu(dot(normed[r], w_ri[...]))

    x_in, d_in, d_in2 = ([], []), ([], []), ([], [])

    def far_in(f, p):
        with jax.named_scope(f"farin{f}{p}"):
            z_in[f][p].wait_recv()
            piece = rows_raw.at[me, f + 1, pieces[p]]
            x_in[f].append(pass_on(piece, to_over))
            d_in[f].append(pass_on(piece, to_mate))

    def far_cross(f, p):
        with jax.named_scope(f"farcross{f}{p}"):
            x_in[f][p].wait_recv()
            d_in2[f].append(pass_on(rows_raw.at[over, f + 1, pieces[p]], to_mate))

    de = {}

    def chip_part(e, j):
        de[j, e].wait_recv()
        return part[e, over if j else me].astype(F32) + de_recv[j, e].astype(F32)

    def expert_first(e):
        with jax.named_scope(f"first{e}"):
            normalize(lambda s: rows_raw[s, e], rows_far.at[e], slice(0, cap))
            hid[e] = twice_gelu(dot(rows_far[e], w_ei[...]))

    def expert_second(e):
        with jax.named_scope(f"second{e}"):
            full = dot(hid[e], w_eo[...])
            for s in range(shards):
                part[e, s] = full[:, s * width:(s + 1) * width].astype(BF16)
            for j, s in ((1, cross), (0, mate)):
                de[j, e] = send(part.at[e, s], de_recv.at[j, e], to_mate)

    xf, zf = ([], []), ([], [])

    def far_out(f):
        with jax.named_scope(f"farout{f}"):
            xf_send[f] = chip_part(f + 1, 1).astype(BF16)
            for r in pieces:
                xf[f].append(send(xf_send.at[f, r], xf_recv.at[f, r], to_over))

    def far_home(f, p):
        r = pieces[p]
        with jax.named_scope(f"farhome{f}{p}"):
            if p == 0:
                de[0, f + 1].wait_recv()
            xf[f][p].wait_recv()
            own = part[f + 1, me, r].astype(F32) + de_recv[0, f + 1, r].astype(F32)
            zf_send[f, r] = (own + xf_recv[f, r].astype(F32)).astype(BF16)
            zf[f].append(send(zf_send.at[f, r], zf_recv.at[f, r], to_far[f]))

    pair_out = {}

    def pair_home(j):
        with jax.named_scope(f"pairhome{j}"):
            pair_send[j] = chip_part(0, j).astype(BF16)
            pair_out[j] = [send(pair_send.at[j, :, c], pair_recv.at[j, :, c], to_pair) for c in lanes]

    dt = ([], [])

    def token_part(j, r):
        with jax.named_scope(f"tokens{j}"):
            both = dot(res_hid[r], w_ro[:, chip_cols(j)])
            for c in range(2):
                tpart[j, c, r] = both[:, c * width:(c + 1) * width].astype(BF16)
            dt[j].append(send(tpart.at[j, 1 - core, r], dt_recv.at[j, r], to_mate))

    def chip_sum(j, c):
        back[j, :cap, c] = gated(pair_recv[j, :, c].astype(F32), 0)
        return dot(take[0], back[j, :, c]) + (tpart[j, core, :, c].astype(F32) + dt_recv[j, :, c].astype(F32))

    def far_wait(f):
        with jax.named_scope(f"farwait{f}"):
            for p in range(last):
                d_in[f][p].wait_recv()
                d_in2[f][p].wait_recv()

    lanes = tuple(slice(lo, lo + 128) for lo in range(0, width, 128))
    last = len(pieces)
    halves = (slice(0, count // 2), slice(count // 2, count))
    tail = len(spans) - 1
    relay(0)
    tok_mate.wait_recv()
    far_in(0, 0)
    for h in range(1, tail):
        relay(h)
        if h == 1:
            for p in range(1, last):
                far_in(0, p)
        residual(h - 1)
    relay(tail)
    with jax.named_scope("pairsend"):
        out_rows2[...] = dot(send_table(pair), tok[over]).astype(BF16)
        pair_in2 = send(out_rows2, rows_raw.at[over, 0], to_pair)
    far_in(1, 0)
    residual(tail - 1)
    for p in range(1, last):
        far_in(1, p)
    for p in range(last):
        far_cross(0, p)
    residual(tail)
    with jax.named_scope("pairrelay"):
        pair_in.wait_recv()
        pair_d = pass_on(rows_raw.at[me, 0], to_mate)
    with jax.named_scope("ownfirst"):
        rows_own[...] = dot(send_table(z), normed[...]).astype(BF16)
        hid_own[...] = twice_gelu(dot(rows_own[...], w_ei[...]))
    with jax.named_scope("pairrelay2"):
        pair_in2.wait_recv()
        pair_d2 = pass_on(rows_raw.at[over, 0], to_mate)
    far_wait(0)
    expert_first(1)
    for p in range(last):
        far_cross(1, p)
    expert_second(1)
    with jax.named_scope("pairwait"):
        pair_d.wait_recv()
        pair_d2.wait_recv()
    expert_first(0)
    expert_second(0)
    far_out(0)
    far_wait(1)
    expert_first(2)
    pair_home(1)
    expert_second(2)
    with jax.named_scope("ownsecond"):
        w_ro[hidden:hidden + cap, :] = gated(dot(hid_own[...], w_eo[...]), 3)
    token_part(1, halves[0])
    far_home(0, 0)
    far_out(1)
    token_part(1, halves[1])
    for p in range(1, last):
        far_home(0, p)
    pair_home(0)
    xt = []
    for k, c in enumerate(lanes):
        with jax.named_scope(f"tokensend{k}"):
            if k == 0:
                for copy in dt[1]:
                    copy.wait_recv()
            pair_out[1][k].wait_recv()
            xt_send[:, c] = chip_sum(1, c).astype(BF16)
            xt.append(send(xt_send.at[:, c], xt_recv.at[:, c], to_over))
    for r in halves:
        token_part(0, r)
    for p in range(last):
        far_home(1, p)
    with jax.named_scope("tokenkeep"):
        for copy in dt[0]:
            copy.wait_recv()
        for k, c in enumerate(lanes):
            pair_out[0][k].wait_recv()
            t_keep[:, c] = chip_sum(0, c)
    for f in range(2):
        with jax.named_scope(f"fartake{f}"):
            for copy in zf[f]:
                copy.wait_recv()
            back[f + 2, :cap] = gated(zf_recv[f].astype(F32), f + 1)
            t_keep[...] = t_keep[...] + dot(take[f + 1], back[f + 2])
    for k, c in enumerate(lanes):
        with jax.named_scope(f"final{k}"):
            xt[k].wait_recv()
            out[:, c] = ((t_keep[:, c] + xt_recv[:, c].astype(F32)) * 0.5).astype(BF16)
    with jax.named_scope("drain"):
        for copy in sent:
            copy.wait_send()


def split_rows(rows, parts):
    step = -(-rows // (16 * parts)) * 16
    return tuple(slice(lo, min(lo + step, rows)) for lo in range(0, rows, step))


def fused(tokens, gain, w_res_in, w_res_out, w_exp_in, w_exp_out, expert_of, slot_of, gate_prob):
    count, width = tokens.shape
    shards = lax.axis_size("mp")
    experts = lax.axis_size("expert")
    cap = max(2, 5 * count // (4 * experts))
    padded = -(-cap // 128) * 128
    model, hidden = w_res_in.shape
    exp_hidden = w_exp_in.shape[2]
    vmem, hbm = pl.BlockSpec(memory_space=pltpu.VMEM), pl.BlockSpec(memory_space=pltpu.HBM)
    buf = lambda *shape: pltpu.VMEM(shape, BF16)
    wide = lambda *shape: pltpu.VMEM(shape, F32)
    spans, pieces = split_rows(count, 4), split_rows(cap, 2)
    copies = 15 + 3 * (width // 128) + 2 * len(spans) + 12 * len(pieces)
    args = (
        tokens, gain[None, :], w_res_in, w_res_out, w_exp_in, w_exp_out, expert_of, slot_of, gate_prob,
    )
    return pl.pallas_call(
        functools.partial(fused_kernel, spans, pieces, cap),
        out_shape=jax.ShapeDtypeStruct((count, width), BF16),
        in_specs=[hbm] * len(args),
        out_specs=vmem,
        scratch_shapes=[
            pltpu.VMEM((count,), jnp.int32), pltpu.VMEM((count,), jnp.int32), wide(count), wide(1, model),
            buf(model, hidden), buf(hidden + padded, model), buf(model, exp_hidden), buf(exp_hidden, model),
            buf(shards, count, width), buf(count, model), buf(count, hidden + padded),
            buf(shards, 3, cap, width), buf(3, cap, width), buf(cap, width),
            buf(cap, model), buf(cap, exp_hidden), buf(3, cap, model), buf(3, cap, exp_hidden),
            buf(3, shards, cap, width), buf(2, 3, cap, width),
            buf(2, cap, width), buf(2, cap, width), buf(2, cap, width), buf(2, cap, width),
            buf(2, cap, width), buf(2, cap, width),
            buf(4, padded, width), buf(3, count, padded), wide(4, cap, 128),
            buf(2, 2, count, width), buf(2, count, width), wide(count, width),
            buf(count, width), buf(count, width), wide(count, 128),
            pltpu.SemaphoreType.DMA((9,)), pltpu.SemaphoreType.DMA((copies,)), pltpu.SemaphoreType.DMA((copies,)),
        ],
        name="fused_layer",
        compiler_params=pltpu.CompilerParams(
            collective_id=0, has_side_effects=True, vmem_limit_bytes=50 * 1024 * 1024
        ),
    )(*(pltpu.with_memory_space_constraint(a, pltpu.HBM) for a in args))


def pick(mesh):
    if mesh.shape["mp"] == 4 and mesh.shape["expert"] == 4:
        return fused
    return per_device


def solution(mesh):
    return jax.shard_map(
        pick(mesh),
        mesh=mesh,
        in_specs=(
            P(("groups", "expert"), "mp"),
            P(),
            P(None, "mp"),
            P("mp", None),
            P("expert", None, "mp"),
            P("expert", "mp", None),
            P(("groups", "expert")),
            P(("groups", "expert")),
            P(("groups", "expert")),
        ),
        out_specs=P(("groups", "expert"), "mp"),
        check_vma=False,
    )
```

time: 46.8 us -> 41.7 us (0.89)
  Pallas kernels: 45.8 us -> 40.8 us
    pallas_call x1, Pallas kernels: 45.8 us -> 40.8 us  [fused(): pl.pallas_call(functools.partial(fused_kernel, spans, pieces, cap), out_s...]
where the time goes in v2:
time: 41.7 us; the launch traced here: 41.5 us
  Pallas kernels  40.8 us (98%)
  local copies, waits for them, and re-layouts  0.75 us (2%)
    pallas_call x1, Pallas kernels, fused(): pl.pallas_call(functools.partial(fused_kernel, spans, pieces, cap), out_s...  40.8 us

profile of v2, /device:TPU:0, one launch (start us, length us, event | category | flops | bytes accessed | tf_op | source)
XLA Modules:
  0.0 41.5 jit_solution(3964010625385435427)
XLA Ops:
  0.0 40.8 %fused_layer.1 = bf16[768,256]{1,0:T(8,128)(2,1)S(1)} custom-call(bf16[768,256]{1,0:T(8,128)(2,1)} %tokens_h.1, f32[1,1024]{1,0:T(1,128)} %bitcast.1, bf16[1024,1024]{1,0:T(8,128)(2,1)} %w_ri_h.1, bf16[1024,1024]{1,0:T(8,128)(2,1)} %w_ro_h.1, bf16[1,1024,1024]{2,1,0:T(8,128)(2,1)} %w_ei_h.1, bf16[1,1024,1024]{2,1,0:T(8,128)(2,1)} %w_eo_h.1, s32[768]{0:T(1024)} %expert_h.1, ...), custom_call_target="tpu_custom_call" | custom-call | tf_op jit(solution)/shard_map/fused_layer/pallas_call | solution.py:405
  40.8 0.7 %copy.11 = bf16[768,256]{1,0:T(8,128)(2,1)} copy(bf16[768,256]{1,0:T(8,128)(2,1)S(1)} %fused_layer.1) | data formatting | bytes 786432

commit v3 on v2

v3 whole, which is shorter than its diff:
```python
import functools

import jax
import jax.numpy as jnp
from jax import lax
from jax.experimental import pallas as pl
from jax.experimental.pallas import tpu as pltpu
from jax.sharding import PartitionSpec as P


def rms_rows(tokens, gain):
    values = tokens.astype(jnp.float32)
    inverse = lax.rsqrt(jnp.mean(values * values, axis=-1, keepdims=True) + 1e-05)
    return (values * inverse * gain).astype(jnp.bfloat16)


def per_device(
    tokens, gain, w_res_in, w_res_out, w_exp_in, w_exp_out, expert_of, slot_of, gate_prob
):
    full_rows = lax.all_gather(tokens, "mp", axis=1, tiled=True)
    normed = rms_rows(full_rows, gain)
    res_hidden = jax.nn.gelu(jnp.dot(normed, w_res_in, preferred_element_type=jnp.float32)).astype(
        jnp.bfloat16
    )
    res_part = jnp.dot(res_hidden, w_res_out, preferred_element_type=jnp.float32)
    row_count = expert_of.shape[0]
    experts = lax.axis_size("expert")
    capacity = max(2, 5 * row_count // (4 * experts))
    feat_width = tokens.shape[1]
    slot_id = jnp.where(slot_of >= 0, expert_of * capacity + slot_of, -1)
    slot_index = jnp.arange(experts * capacity, dtype=jnp.int32)
    send_table = (slot_index[:, None] == slot_id[None, :]).astype(jnp.bfloat16)
    take_table = (slot_id[:, None] == slot_index[None, :]).astype(jnp.bfloat16)
    local_in = w_exp_in[0]
    local_out = w_exp_out[0]
    mp_index = lax.axis_index("mp")
    own_slice = lax.dynamic_slice_in_dim(normed, mp_index * feat_width, feat_width, 1)
    outgoing = jnp.dot(send_table, own_slice, preferred_element_type=jnp.float32).astype(
        jnp.bfloat16
    )
    incoming = lax.all_to_all(
        outgoing.reshape(experts, capacity, feat_width),
        "expert",
        split_axis=0,
        concat_axis=0,
        tiled=True,
    )
    piece = lax.all_gather(incoming, "mp", axis=2, tiled=True)
    flat_piece = piece.reshape(-1, piece.shape[2])
    preact = jnp.dot(flat_piece, local_in, preferred_element_type=jnp.float32)
    exp_hidden = jax.nn.gelu(preact).astype(jnp.bfloat16)
    exp_part = jnp.dot(exp_hidden, local_out, preferred_element_type=jnp.float32)
    gate_column = gate_prob[:, None]
    summed = lax.psum_scatter(exp_part.astype(jnp.bfloat16), "mp", scatter_dimension=1, tiled=True)
    returned = lax.all_to_all(
        summed.reshape(experts, capacity, feat_width),
        "expert",
        split_axis=0,
        concat_axis=0,
        tiled=True,
    )
    moe_value = jnp.dot(
        take_table,
        returned.reshape(experts * capacity, feat_width),
        preferred_element_type=jnp.float32,
    )
    res_sum = lax.psum_scatter(
        res_part.astype(jnp.bfloat16), "mp", scatter_dimension=1, tiled=True
    ).astype(jnp.float32)
    return (res_sum + gate_column * moe_value).astype(jnp.bfloat16)


MESH = pl.DeviceIdType.MESH
F32 = jnp.float32
BF16 = jnp.bfloat16
ORDER = (
    ("ag", 0), ("ag", 1), ("ag", 2), ("ag", 3), ("mate",), ("s", 0), ("sp",), ("s", 1), ("cols",), ("near",),
    ("relay", 0), ("zi", 0, 0), ("relay", 1), ("zi", 0, 1), ("res", 0), ("relay", 2), ("res", 1), ("relay", 3),
    ("psend",), ("zi", 1, 0), ("res", 2), ("own",), ("zi", 1, 1), ("xc", 0, 0), ("xc", 0, 1), ("res", 3),
    ("pr1",), ("own1",), ("pr2",), ("first", 1), ("xc", 1, 0), ("xc", 1, 1), ("second", 1), ("first", 0),
    ("second", 0), ("fo", 0), ("first", 2), ("ph", 1), ("second", 2), ("own2",), ("tk", 1, 0), ("fo", 1),
    ("fh", 0, 0), ("tk", 1, 1), ("fh", 0, 1), ("ph", 0), ("ts", 0), ("ts", 1), ("tk", 0, 0), ("fh", 1, 0),
    ("tk", 0, 1), ("fh", 1, 1), ("tkeep",), ("ft", 0), ("ft", 1), ("fin",),
)


def dot(a, b):
    return jnp.dot(a, b, preferred_element_type=F32)


def twice_gelu(x):
    bent = x * (0.7978845608028654 + 0.035677408136300125 * (x * x))
    return (x + x * jnp.tanh(bent)).astype(BF16)


def fused_kernel(
    spans, pieces, cap, tokens_h, gain_h, w_ri_h, w_ro_h, w_ei_h, w_eo_h, expert_h, slot_h, gate_h, out,
    expert_v, slot_v, gate_v, gain, w_ri, w_ro, w_ei, w_eo, tok, res_hid, rows_raw, out_rows, out_rows2,
    own_table, hid, part, de_recv, pair_send, pair_recv, xf_send, xf_recv, zf_send, zf_recv,
    back, take, slot_gate, tpart, dt_recv, t_keep, xt_send, xt_recv, id_col, load_sem, send_sem, recv_sem,
):
    count, width = out.shape
    shards = tok.shape[1] // width
    padded = take.shape[2]
    hidden = res_hid.shape[1] - padded
    me = lax.axis_index("mp")
    z = lax.axis_index("expert")
    core = lax.rem(me, 2)
    chip = me // 2
    over = lax.rem(me + 2, 4)
    mate = me + 1 - 2 * core
    cross = lax.rem(mate + 2, 4)
    pair = z + 1 - 2 * lax.rem(z, 2)
    far = (lax.rem(z + 2, 4), 3 - z)
    to_over, to_mate, to_pair = {"mp": over}, {"mp": mate}, {"expert": pair}
    to_far = ({"expert": far[0]}, {"expert": far[1]})

    barrier = pltpu.get_barrier_semaphore()
    for dest in (to_over, to_mate, to_pair, to_far[0], to_far[1]):
        pl.semaphore_signal(barrier, inc=1, device_id=dest, device_id_type=MESH)

    def cols(shard):
        return pl.ds(pl.multiple_of(shard * width, width), width)

    loads = []
    for k, (src, dst) in enumerate((
        (expert_h, expert_v), (slot_h, slot_v), (tokens_h, tok.at[:, cols(me)]), (gate_h, gate_v), (gain_h, gain),
        (w_ri_h, w_ri), (w_ei_h.at[0], w_ei), (w_eo_h.at[0], w_eo), (w_ro_h, w_ro.at[:hidden]),
    )):
        load = pltpu.make_async_copy(src, dst, load_sem.at[k])
        load.start()
        loads.append(load)

    sent = []

    def send(src, dst, dest):
        k = len(sent)
        copy = pltpu.make_async_remote_copy(
            src_ref=src, dst_ref=dst, send_sem=send_sem.at[k], recv_sem=recv_sem.at[k],
            device_id=dest, device_id_type=MESH,
        )
        copy.start()
        sent.append(copy)
        return copy

    def pass_on(ref, dest):
        return send(ref, ref, dest)

    def send_table(e):
        base = (e * cap).astype(F32)
        return jnp.where(slot_rows + base == ids, 1.0, 0.0).astype(BF16)

    def chip_cols(j):
        block = chip if j == 0 else 1 - chip
        return pl.ds(pl.multiple_of(block * 2 * width, 2 * width), 2 * width)

    def first_layer(rows, w_ref):
        values = rows.astype(F32)
        mean = jnp.mean(values * values, axis=-1, keepdims=True)
        return twice_gelu(dot(rows, w_ref[...]) * lax.rsqrt(mean + 1e-05))

    with jax.named_scope("entry"):
        loads[0].wait()
        loads[1].wait()
        expert_row = expert_v[...].reshape(1, count)
        slot_row = slot_v[...].reshape(1, count)
        ids = jnp.where(slot_row >= 0, expert_row * cap + slot_row, -1).astype(F32)
        slot_rows = lax.broadcasted_iota(jnp.int32, (cap, count), 0).astype(F32)
        loads[2].wait()
    with jax.named_scope("barrier"):
        pl.semaphore_wait(barrier, 5)

    arrive = {}
    waited = set()

    def await_all(*names):
        for name in names:
            if name not in waited:
                waited.add(name)
                arrive[name].wait_recv()

    def tables():
        loads[3].wait()
        gate_row = gate_v[...].reshape(1, count)
        id_col[...] = jnp.broadcast_to(ids, (128, count)).T
        lane = lax.broadcasted_iota(jnp.int32, (count, 128), 1).astype(F32)
        for k, e in enumerate((pair, far[0], far[1], z)):
            base = (e * cap).astype(F32)
            gates = jnp.sum(jnp.where(slot_rows + base == ids, gate_row, 0.0), axis=1, keepdims=True)
            slot_gate[k] = jnp.broadcast_to(gates, (cap, 128))
            for lo in range(0, padded, 128):
                hit = jnp.where(lane + (base + lo) == id_col[...], 1.0, 0.0).astype(BF16)
                if k < 3:
                    take[k, :, lo:lo + 128] = hit
                else:
                    res_hid[:, hidden + lo:hidden + lo + 128] = hit
        back[:, cap:, :] = jnp.zeros((4, padded - cap, width), BF16)
        for k in range(4, 9):
            loads[k].wait()
        gain_col = jnp.broadcast_to(gain[...], (128, shards * width)).T
        for w_ref in (w_ri, w_ei):
            for lo in range(0, w_ref.shape[1], 128):
                w_ref[:, lo:lo + 128] = (w_ref[:, lo:lo + 128].astype(F32) * gain_col).astype(BF16)
        w_ro[hidden + cap:, :] = jnp.zeros((padded - cap, shards * width), BF16)

    def gated(rows, k):
        scale = slot_gate[k]
        return (rows * jnp.concatenate([scale] * (rows.shape[1] // 128), axis=1)).astype(BF16)

    lanes = tuple(slice(lo, lo + 128) for lo in range(0, width, 128))
    halves = (slice(0, count // 2), slice(count // 2, count))
    parts = range(len(pieces))

    def gather(h):
        arrive["over", h] = pass_on(tok.at[spans[h], cols(me)], to_over)

    def gather_mate():
        arrive["mate"] = pass_on(tok.at[:, cols(me)], to_mate)

    def far_send(f):
        out_rows[f + 1] = dot(send_table(far[f]), tok[:, cols(me)]).astype(BF16)
        for p, r in enumerate(pieces):
            arrive["z", f, p] = send(out_rows.at[f + 1, r], rows_raw.at[f + 1, r, cols(me)], to_far[f])

    def pair_send_own():
        out_rows[0] = dot(send_table(pair), tok[:, cols(me)]).astype(BF16)
        arrive["pair"] = send(out_rows.at[0], rows_raw.at[0, :, cols(me)], to_pair)

    def relay(h):
        await_all(("over", h))
        arrive["cross", h] = pass_on(tok.at[spans[h], cols(over)], to_mate)

    def residual(h):
        r = spans[h]
        await_all("mate", ("cross", h))
        res_hid[r, :hidden] = first_layer(tok[r], w_ri)

    def pair_send_over():
        out_rows2[...] = dot(send_table(pair), tok[:, cols(over)]).astype(BF16)
        arrive["pair2"] = send(out_rows2, rows_raw.at[0, :, cols(over)], to_pair)

    def far_in(f, p):
        await_all(("z", f, p))
        piece = rows_raw.at[f + 1, pieces[p], cols(me)]
        arrive["x", f, p] = pass_on(piece, to_over)
        arrive["near", f, p] = pass_on(piece, to_mate)

    def far_cross(f, p):
        await_all(("x", f, p))
        arrive["far", f, p] = pass_on(rows_raw.at[f + 1, pieces[p], cols(over)], to_mate)

    def pair_relay(k, s):
        await_all("pair2" if k else "pair")
        arrive["pairmate", k] = pass_on(rows_raw.at[0, :, cols(s)], to_mate)

    def expert_first(e):
        if e == 0:
            await_all(("pairmate", 0), ("pairmate", 1))
        else:
            await_all(*((kind, e - 1, p) for kind in ("near", "far") for p in parts))
        hid[e] = first_layer(rows_raw[e], w_ei)

    def expert_second(e):
        full = dot(hid[e], w_eo[...])
        for s in range(shards):
            part[e, s] = full[:, s * width:(s + 1) * width].astype(BF16)
        for j, s in ((1, cross), (0, mate)):
            arrive["part", j, e] = send(part.at[e, s], de_recv.at[j, e], to_mate)

    def chip_part(e, j, r):
        await_all(("part", j, e))
        return part[e, over if j else me, r].astype(F32) + de_recv[j, e, r].astype(F32)

    def own_rows(*shard_ids):
        for s in shard_ids:
            rows_raw[3, :, cols(s)] = dot(own_table[...], tok[:, cols(s)]).astype(BF16)

    def own_near():
        own_table[...] = send_table(z)
        await_all("mate")
        own_rows(me, mate)

    def own_first():
        own_rows(cross)
        hid[3] = first_layer(rows_raw[3], w_ei)

    def own_second():
        w_ro[hidden:hidden + cap, :] = gated(dot(hid[3], w_eo[...]), 3)

    def far_out(f):
        xf_send[f] = chip_part(f + 1, 1, slice(0, cap)).astype(BF16)
        for p, r in enumerate(pieces):
            arrive["xf", f, p] = send(xf_send.at[f, r], xf_recv.at[f, r], to_over)

    def far_home(f, p):
        r = pieces[p]
        own = chip_part(f + 1, 0, r)
        await_all(("xf", f, p))
        zf_send[f, r] = (own + xf_recv[f, r].astype(F32)).astype(BF16)
        arrive["zf", f, p] = send(zf_send.at[f, r], zf_recv.at[f, r], to_far[f])

    def pair_home(j):
        pair_send[j] = chip_part(0, j, slice(0, cap)).astype(BF16)
        for k, c in enumerate(lanes):
            arrive["back", j, k] = send(pair_send.at[j, :, c], pair_recv.at[j, :, c], to_pair)

    def token_part(j, i):
        r = halves[i]
        both = dot(res_hid[r], w_ro[:, chip_cols(j)])
        for c in range(2):
            tpart[j, c, r] = both[:, c * width:(c + 1) * width].astype(BF16)
        arrive["tok", j, i] = send(tpart.at[j, 1 - core, r], dt_recv.at[j, r], to_mate)

    def chip_sum(j, k):
        c = lanes[k]
        await_all(("tok", j, 0), ("tok", j, 1), ("back", j, k))
        back[j, :cap, c] = gated(pair_recv[j, :, c].astype(F32), 0)
        return dot(take[0], back[j, :, c]) + (tpart[j, core, :, c].astype(F32) + dt_recv[j, :, c].astype(F32))

    def token_send(k):
        c = lanes[k]
        xt_send[:, c] = chip_sum(1, k).astype(BF16)
        arrive["xt", k] = send(xt_send.at[:, c], xt_recv.at[:, c], to_over)

    def token_keep():
        for k, c in enumerate(lanes):
            t_keep[:, c] = chip_sum(0, k)

    def far_take(f):
        await_all(*(("zf", f, p) for p in parts))
        back[f + 2, :cap] = gated(zf_recv[f].astype(F32), f + 1)
        t_keep[...] = t_keep[...] + dot(take[f + 1], back[f + 2])

    def finish():
        for k, c in enumerate(lanes):
            await_all(("xt", k))
            out[:, c] = ((t_keep[:, c] + xt_recv[:, c].astype(F32)) * 0.5).astype(BF16)
        for copy in sent:
            copy.wait_send()

    steps = {
        "ag": gather, "mate": gather_mate, "s": far_send, "sp": pair_send_own, "cols": tables, "relay": relay,
        "res": residual, "psend": pair_send_over, "zi": far_in, "xc": far_cross, "own1": own_first, "near": own_near, "own": lambda: own_rows(over),
        "own2": own_second, "fo": far_out, "fh": far_home, "ph": pair_home, "tk": token_part, "ts": token_send,
        "tkeep": token_keep, "ft": far_take, "fin": finish, "first": expert_first, "second": expert_second,
        "pr1": lambda: pair_relay(0, me), "pr2": lambda: pair_relay(1, over),
    }
    for step in ORDER:
        with jax.named_scope("".join(map(str, step))):
            steps[step[0]](*step[1:])


def split_rows(rows, parts):
    step = -(-rows // (16 * parts)) * 16
    return tuple(slice(lo, min(lo + step, rows)) for lo in range(0, rows, step))


def fused(tokens, gain, w_res_in, w_res_out, w_exp_in, w_exp_out, expert_of, slot_of, gate_prob):
    count, width = tokens.shape
    shards = lax.axis_size("mp")
    experts = lax.axis_size("expert")
    cap = max(2, 5 * count // (4 * experts))
    padded = -(-cap // 128) * 128
    model, hidden = w_res_in.shape
    exp_hidden = w_exp_in.shape[2]
    vmem, hbm = pl.BlockSpec(memory_space=pltpu.VMEM), pl.BlockSpec(memory_space=pltpu.HBM)
    buf = lambda *shape: pltpu.VMEM(shape, BF16)
    wide = lambda *shape: pltpu.VMEM(shape, F32)
    spans, pieces = split_rows(count, 4), split_rows(cap, 2)
    copies = 15 + 3 * (width // 128) + 2 * len(spans) + 12 * len(pieces)
    args = (
        tokens, gain[None, :], w_res_in, w_res_out, w_exp_in, w_exp_out, expert_of, slot_of, gate_prob,
    )
    return pl.pallas_call(
        functools.partial(fused_kernel, spans, pieces, cap),
        out_shape=jax.ShapeDtypeStruct((count, width), BF16),
        in_specs=[hbm] * len(args),
        out_specs=vmem,
        scratch_shapes=[
            pltpu.VMEM((count,), jnp.int32), pltpu.VMEM((count,), jnp.int32), wide(count), wide(1, model),
            buf(model, hidden), buf(hidden + padded, model), buf(model, exp_hidden), buf(exp_hidden, model),
            buf(count, model), buf(count, hidden + padded),
            buf(4, cap, model), buf(3, cap, width), buf(cap, width),
            buf(cap, count), buf(4, cap, exp_hidden),
            buf(3, shards, cap, width), buf(2, 3, cap, width),
            buf(2, cap, width), buf(2, cap, width), buf(2, cap, width), buf(2, cap, width),
            buf(2, cap, width), buf(2, cap, width),
            buf(4, padded, width), buf(3, count, padded), wide(4, cap, 128),
            buf(2, 2, count, width), buf(2, count, width), wide(count, width),
            buf(count, width), buf(count, width), wide(count, 128),
            pltpu.SemaphoreType.DMA((9,)), pltpu.SemaphoreType.DMA((copies,)), pltpu.SemaphoreType.DMA((copies,)),
        ],
        name="fused_layer",
        compiler_params=pltpu.CompilerParams(
            collective_id=0, has_side_effects=True, vmem_limit_bytes=50 * 1024 * 1024
        ),
    )(*(pltpu.with_memory_space_constraint(a, pltpu.HBM) for a in args))


def pick(mesh):
    if mesh.shape["mp"] == 4 and mesh.shape["expert"] == 4:
        return fused
    return per_device


def solution(mesh):
    return jax.shard_map(
        pick(mesh),
        mesh=mesh,
        in_specs=(
            P(("groups", "expert"), "mp"),
            P(),
            P(None, "mp"),
            P("mp", None),
            P("expert", None, "mp"),
            P("expert", "mp", None),
            P(("groups", "expert")),
            P(("groups", "expert")),
            P(("groups", "expert")),
        ),
        out_specs=P(("groups", "expert"), "mp"),
        check_vma=False,
    )
```

time: 41.7 us -> 41.1 us (0.986)
  Pallas kernels: 40.8 us -> 40.1 us
    pallas_call x1, Pallas kernels: 40.8 us -> 40.1 us  [fused(): pl.pallas_call(functools.partial(fused_kernel, spans, pieces, cap), out_s...]
where the time goes in v3:
time: 41.1 us; the launch traced here: 40.9 us
  Pallas kernels  40.1 us (98%)
  local copies, waits for them, and re-layouts  0.75 us (2%)
    pallas_call x1, Pallas kernels, fused(): pl.pallas_call(functools.partial(fused_kernel, spans, pieces, cap), out_s...  40.1 us

profile of v3, /device:TPU:0, one launch (start us, length us, event | category | flops | bytes accessed | tf_op | source)
XLA Modules:
  0.0 40.9 jit_solution(3758571948046604760)
XLA Ops:
  0.0 40.1 %fused_layer.1 = bf16[768,256]{1,0:T(8,128)(2,1)S(1)} custom-call(bf16[768,256]{1,0:T(8,128)(2,1)} %tokens_h.1, f32[1,1024]{1,0:T(1,128)} %bitcast.1, bf16[1024,1024]{1,0:T(8,128)(2,1)} %w_ri_h.1, bf16[1024,1024]{1,0:T(8,128)(2,1)} %w_ro_h.1, bf16[1,1024,1024]{2,1,0:T(8,128)(2,1)} %w_ei_h.1, bf16[1,1024,1024]{2,1,0:T(8,128)(2,1)} %w_eo_h.1, s32[768]{0:T(1024)} %expert_h.1, ...), custom_call_target="tpu_custom_call" | custom-call | tf_op jit(solution)/shard_map/fused_layer/pallas_call | solution.py:374
  40.1 0.7 %copy.11 = bf16[768,256]{1,0:T(8,128)(2,1)} copy(bf16[768,256]{1,0:T(8,128)(2,1)S(1)} %fused_layer.1) | data formatting | bytes 786432

commit v4 on v3

--- a/solution.py
+++ b/solution.py
@@ -166,6 +166,7 @@
         slot_row = slot_v[...].reshape(1, count)
         ids = jnp.where(slot_row >= 0, expert_row * cap + slot_row, -1).astype(F32)
         slot_rows = lax.broadcasted_iota(jnp.int32, (cap, count), 0).astype(F32)
+        own_table[...] = send_table(far[0])
         loads[2].wait()
     with jax.named_scope("barrier"):
         pl.semaphore_wait(barrier, 5)
@@ -218,7 +219,8 @@
         arrive["mate"] = pass_on(tok.at[:, cols(me)], to_mate)
 
     def far_send(f):
-        out_rows[f + 1] = dot(send_table(far[f]), tok[:, cols(me)]).astype(BF16)
+        table = own_table[...] if f == 0 else send_table(far[f])
+        out_rows[f + 1] = dot(table, tok[:, cols(me)]).astype(BF16)
         for p, r in enumerate(pieces):
             arrive["z", f, p] = send(out_rows.at[f + 1, r], rows_raw.at[f + 1, r, cols(me)], to_far[f])
 

time: 41.1 us -> 41.1 us (level)
  no operation moved by 1% of the time
where the time goes in v4:
time: 41.1 us; the launch traced here: 40.9 us
  Pallas kernels  40.1 us (98%)
  local copies, waits for them, and re-layouts  0.75 us (2%)
    pallas_call x1, Pallas kernels, fused(): pl.pallas_call(functools.partial(fused_kernel, spans, pieces, cap), out_s...  40.1 us

profile of v4, /device:TPU:0, one launch (start us, length us, event | category | flops | bytes accessed | tf_op | source)
XLA Modules:
  0.0 40.9 jit_solution(3894405378657803297)
XLA Ops:
  0.0 40.1 %fused_layer.1 = bf16[768,256]{1,0:T(8,128)(2,1)S(1)} custom-call(bf16[768,256]{1,0:T(8,128)(2,1)} %tokens_h.1, f32[1,1024]{1,0:T(1,128)} %bitcast.1, bf16[1024,1024]{1,0:T(8,128)(2,1)} %w_ri_h.1, bf16[1024,1024]{1,0:T(8,128)(2,1)} %w_ro_h.1, bf16[1,1024,1024]{2,1,0:T(8,128)(2,1)} %w_ei_h.1, bf16[1,1024,1024]{2,1,0:T(8,128)(2,1)} %w_eo_h.1, s32[768]{0:T(1024)} %expert_h.1, ...), custom_call_target="tpu_custom_call" | custom-call | tf_op jit(solution)/shard_map/fused_layer/pallas_call | solution.py:376
  40.1 0.7 %copy.11 = bf16[768,256]{1,0:T(8,128)(2,1)} copy(bf16[768,256]{1,0:T(8,128)(2,1)S(1)} %fused_layer.1) | data formatting | bytes 786432
